TPU v7x, 256 devices: a whole 4x4x8 slice. The times are simulated.
256 devices in a mesh: rows: 8 (over x_hi, y), cols: 32 (over z, x_lo, core).
Axes of the slice: x: 4 (x_hi: 2, x_lo: 2; x = x_hi * 2 + x_lo), y: 4, z: 8, core: 2. Of those that a mesh axis runs over, the one named last changes fastest.
Arguments:
- features: bfloat16 [4, 256, 64, 4096], P(None, None, 'rows', 'cols'), may hold values from -8 to 8
- cotangent: bfloat16 [4, 256, 64, 4096], P(None, None, 'rows', 'cols'), may hold values from -6 to 6
- reduce_weight: bfloat16 [256, 64], replicated, may hold values from -0.375 to 0.375
- spatial_weight: bfloat16 [9, 64, 64], replicated, may hold values from -0.25 to 0.25
- expand_weight: bfloat16 [64, 256], replicated, may hold values from -0.75 to 0.75
- reduce_factor: float32 [4, 256], replicated, may hold values from 0.25 to 1.75
- spatial_factor: float32 [4, 64], replicated, may hold values from 0.25 to 1.75
- expand_factor: float32 [4, 64], replicated, may hold values from 0.25 to 1.75
- output_factor: float32 [4, 256], replicated, may hold values from 0.25 to 1.75
- gain_first: float32 [64], replicated, may hold values from 0.25 to 1.75
- shift_first: float32 [64], replicated, may hold values from -3 to 3
- gain_second: float32 [64], replicated, may hold values from 0.25 to 1.75
- shift_second: float32 [64], replicated, may hold values from -3 to 3
Outputs:
- grad_features: bfloat16 [4, 256, 64, 4096], P(None, None, 'rows', 'cols')
- grad_reduce: float32 [256, 64], replicated
- grad_spatial: float32 [9, 64, 64], replicated
- grad_expand: float32 [64, 256], replicated
- grad_reduce_factor: float32 [4, 256], replicated
- grad_spatial_factor: float32 [4, 64], replicated
- grad_expand_factor: float32 [4, 64], replicated
- grad_output_factor: float32 [4, 256], replicated
- grad_gain_first: float32 [64], replicated
- grad_shift_first: float32 [64], replicated
- grad_gain_second: float32 [64], replicated
- grad_shift_second: float32 [64], replicated
All inputs are finite; a program needn't handle non-finite values.
Results may differ from a plain program's by a relative error of at most 0.01.
Values may be sent and summed in bfloat16 or wider, within the bound.
A program may use at most 128 MiB of HBM per device.

v0:
```python
import functools
import jax
import jax.numpy as jnp
from jax import lax
from jax.sharding import Mesh
from jax.sharding import PartitionSpec as P

ROWS_COLS = ("rows_0", "rows_1", "cols_0", "cols_1", "cols_2")
ROWS = ("rows_0", "rows_1")
COLS = ("cols_0", "cols_1", "cols_2")
EPSILON = 1e-05


def by_axis(array, axes):
    return functools.reduce(lax.psum, axes, array)


def with_halo(cells, sides, width):
    for axis, dim in sides:
        count = lax.axis_size(axis)
        ends = count - 1
        head = lax.slice_in_dim(cells, 0, width, axis=dim)
        tail = lax.slice_in_dim(cells, cells.shape[dim] - width, cells.shape[dim], axis=dim)
        cells = jnp.concatenate(
            [
                lax.ppermute(tail, axis, [(i, (i + 1) % count) for i in range(ends)]),
                cells,
                lax.ppermute(head, axis, [((i + 1) % count, i) for i in range(ends)]),
            ],
            axis=dim,
        )
    return cells


def packed_total(arrays, axis):
    flat, at, finished = (jnp.concatenate([a.reshape(-1) for a in arrays]), 0, [])
    so_far = lax.psum(flat, axis)
    for a in arrays:
        finished.append(so_far[at : at + a.size].reshape(a.shape))
        at += a.size
    return tuple(finished)


def activate(value):
    return value * jax.nn.sigmoid(value)


def slope(value):
    sig = jax.nn.sigmoid(value)
    return sig * (1.0 + value * (1.0 - sig))


def norm_forward(acts, gain, shift, count):
    total, square = (
        by_axis(jnp.sum(acts, axis=2), ROWS_COLS),
        by_axis(jnp.sum(acts * acts, axis=2), ROWS_COLS),
    )
    mean = total / count
    var = square / count - mean * mean
    centred = acts - mean[:, :, None]
    rstd = lax.rsqrt(var + EPSILON)[:, :, None]
    normed = centred * rstd
    pre = gain[None, :, None] * normed + shift[None, :, None]
    return (activate(pre).astype(jnp.bfloat16), normed, pre, rstd)


def norm_backward(upstream, normed, pre, rstd, gain, count):
    dpre = upstream * slope(pre)
    plain, weighted = (
        by_axis(jnp.sum(dpre, axis=2), ROWS_COLS),
        by_axis(jnp.sum(dpre * normed, axis=2), ROWS_COLS),
    )
    dact = (
        gain[None, :, None]
        * rstd
        * (dpre - plain[:, :, None] / count - normed * weighted[:, :, None] / count)
    )
    return (dact, jnp.sum(weighted, axis=0), jnp.sum(plain, axis=0))


def rim_cells(field):
    return with_halo(field, ((ROWS, 2), (COLS, 3)), 1)


def rim_grads(field):
    return with_halo(field, ((ROWS, 2), (COLS, 3)), 1)


def conv_forward(padded, weights, tall, broad):
    members, narrow = (padded.shape[0], padded.shape[1])
    total = None
    for tap in range(9):
        row_off, col_off = (tap // 3, tap % 3)
        window = padded[:, :, row_off : row_off + tall, col_off : col_off + broad].reshape(
            members, narrow, tall * broad
        )
        term = jnp.einsum(
            "mfo,mfp->mop", weights[:, tap], window, preferred_element_type=jnp.float32
        )
        total = term if total is None else total + term
    return total


def conv_backward(padded_back, padded_one, weights, dact_low, tall, broad):
    members, narrow = (padded_back.shape[0], padded_back.shape[1])
    total = None
    pieces = []
    for tap in range(9):
        row_off, col_off = (tap // 3, tap % 3)
        flipped = padded_back[
            :, :, 2 - row_off : 2 - row_off + tall, 2 - col_off : 2 - col_off + broad
        ].reshape(members, narrow, tall * broad)
        term = jnp.einsum(
            "mfo,mop->mfp", weights[:, tap], flipped, preferred_element_type=jnp.float32
        )
        total = term if total is None else total + term
        window = padded_one[:, :, row_off : row_off + tall, col_off : col_off + broad].reshape(
            members, narrow, tall * broad
        )
        pieces.append(
            jnp.einsum("mfp,mop->mfo", window, dact_low, preferred_element_type=jnp.float32)
        )
    return (total, jnp.stack(pieces, axis=1))


def fold_members(
    part_reduce,
    part_spatial,
    part_expand,
    rw,
    sw,
    ew,
    reduce_factor,
    spatial_factor,
    expand_factor,
    output_factor,
):
    grad_reduce = jnp.sum(part_reduce * reduce_factor[:, :, None], axis=0)
    grad_reduce_factor = jnp.sum(part_reduce * rw[None], axis=2)
    grad_spatial = jnp.sum(part_spatial * spatial_factor[:, None, :, None], axis=0)
    grad_spatial_factor = jnp.sum(part_spatial * sw[None], axis=(1, 3))
    grad_expand = jnp.sum(
        part_expand * expand_factor[:, :, None] * output_factor[:, None, :], axis=0
    )
    grad_expand_factor = jnp.sum(part_expand * ew[None] * output_factor[:, None, :], axis=2)
    grad_output_factor = jnp.sum(part_expand * ew[None] * expand_factor[:, :, None], axis=1)
    return (
        grad_reduce,
        grad_spatial,
        grad_expand,
        grad_reduce_factor,
        grad_spatial_factor,
        grad_expand_factor,
        grad_output_factor,
    )


def body(
    features,
    cotangent,
    reduce_weight,
    spatial_weight,
    expand_weight,
    reduce_factor,
    spatial_factor,
    expand_factor,
    output_factor,
    gain_first,
    shift_first,
    gain_second,
    shift_second,
):
    members, channels, tall, broad = features.shape
    narrow = reduce_weight.shape[1]
    cells = tall * broad
    count = float(cells * lax.axis_size(ROWS) * lax.axis_size(COLS))
    rw = reduce_weight.astype(jnp.float32)
    sw = spatial_weight.astype(jnp.float32)
    ew = expand_weight.astype(jnp.float32)
    member_reduce = (reduce_factor[:, :, None] * rw[None]).astype(jnp.bfloat16)
    member_spatial = (spatial_factor[:, None, :, None] * sw[None]).astype(jnp.bfloat16)
    member_expand = (expand_factor[:, :, None] * ew[None] * output_factor[:, None, :]).astype(
        jnp.bfloat16
    )
    flat = features.reshape(members, channels, cells)
    first = jnp.einsum("mcf,mcp->mfp", member_reduce, flat, preferred_element_type=jnp.float32)
    hidden_one, normed_one, pre_one, rstd_one = norm_forward(first, gain_first, shift_first, count)
    padded_one = rim_cells(hidden_one.reshape(members, narrow, tall, broad))
    second = conv_forward(padded_one, member_spatial, tall, broad)
    hidden_two, normed_two, pre_two, rstd_two = norm_forward(
        second, gain_second, shift_second, count
    )
    third = jnp.einsum(
        "mfc,mfp->mcp", member_expand, hidden_two, preferred_element_type=jnp.float32
    )
    summed = flat.astype(jnp.float32) + third
    upstream = cotangent.reshape(members, channels, cells).astype(jnp.float32) * slope(summed)
    upstream_low = upstream.astype(jnp.bfloat16)
    back_two = jnp.einsum(
        "mfc,mcp->mfp", member_expand, upstream_low, preferred_element_type=jnp.float32
    )
    part_expand = jnp.einsum(
        "mfp,mcp->mfc", hidden_two, upstream_low, preferred_element_type=jnp.float32
    )
    dact_two, grad_gain_second, grad_shift_second = norm_backward(
        back_two, normed_two, pre_two, rstd_two, gain_second, count
    )
    dact_two_low = dact_two.astype(jnp.bfloat16)
    padded_back = rim_grads(dact_two_low.reshape(members, narrow, tall, broad))
    back_one, part_spatial = conv_backward(
        padded_back, padded_one, member_spatial, dact_two_low, tall, broad
    )
    dact_one, grad_gain_first, grad_shift_first = norm_backward(
        back_one, normed_one, pre_one, rstd_one, gain_first, count
    )
    dact_one_low = dact_one.astype(jnp.bfloat16)
    grad_flat = upstream + jnp.einsum(
        "mcf,mfp->mcp", member_reduce, dact_one_low, preferred_element_type=jnp.float32
    )
    grad_features = grad_flat.astype(jnp.bfloat16).reshape(members, channels, tall, broad)
    part_reduce = jnp.einsum("mcp,mfp->mcf", flat, dact_one_low, preferred_element_type=jnp.float32)
    local = fold_members(
        part_reduce,
        part_spatial,
        part_expand,
        rw,
        sw,
        ew,
        reduce_factor,
        spatial_factor,
        expand_factor,
        output_factor,
    )
    totals = packed_total(
        (local[0], local[1], local[2], local[3], local[4], local[5], local[6]), ROWS_COLS
    )
    return (
        grad_features,
        totals[0],
        totals[1],
        totals[2],
        totals[3],
        totals[4],
        totals[5],
        totals[6],
        grad_gain_first,
        grad_shift_first,
        grad_gain_second,
        grad_shift_second,
    )


def solution(mesh):
    split = Mesh(
        mesh.devices.reshape(2, 4, 8, 2, 2), ("rows_0", "rows_1", "cols_0", "cols_1", "cols_2")
    )
    placed = (
        P(None, None, ROWS, COLS),
        P(None, None, ROWS, COLS),
        P(),
        P(),
        P(),
        P(),
        P(),
        P(),
        P(),
        P(),
        P(),
        P(),
        P(),
    )
    return jax.shard_map(
        body,
        mesh=split,
        in_specs=placed,
        out_specs=(
            P(None, None, ROWS, COLS),
            P(),
            P(),
            P(),
            P(),
            P(),
            P(),
            P(),
            P(),
            P(),
            P(),
            P(),
        ),
        check_vma=False,
    )
```

profile of v0, /device:TPU:1, one launch (start us, length us, event | category | flops | bytes accessed | tf_op | source)
XLA Modules:
  0.0 572.1 jit_solution(7597058974139156140)
XLA Ops:
  10.8 5.9 %all-reduce.19 = (f32[4,64]{1,0:T(4,128)S(1)}, f32[4,64]{1,0:T(4,128)S(1)}) all-reduce(f32[4,64]{1,0:T(4,128)S(1)} %get-tuple-element.57, f32[4,64]{1,0:T(4,128)S(1)} %get-tuple-element.56), channel_id=1, replica_groups=mesh['rows_0'=2,'rows_1'=4,'cols_0'=8,'cols_1'=2,'cols_2'=2] {'rows_0'}, use_global_device_ids=true, to_apply=%region_7.0 | all-reduce | flops 512 | bytes 4096 | tf_op jit(solution)/shard_map/psum | solution.py:15
  16.6 8.9 %all-reduce.7 = (f32[4,64]{1,0:T(4,128)S(1)}, f32[4,64]{1,0:T(4,128)S(1)}) all-reduce(f32[4,64]{1,0:T(4,128)S(1)} %get-tuple-element.101, f32[4,64]{1,0:T(4,128)S(1)} %get-tuple-element.102), channel_id=1, replica_groups=mesh['rows_0'=2,'rows_1'=4,'cols_0'=8,'cols_1'=2,'cols_2'=2] {'rows_1'}, use_global_device_ids=true, to_apply=%region_8.0 | all-reduce | flops 512 | bytes 4096 | tf_op jit(solution)/shard_map/psum | solution.py:15
  25.6 16.2 %all-reduce.3 = (f32[4,64]{1,0:T(4,128)S(1)}, f32[4,64]{1,0:T(4,128)S(1)}) all-reduce(f32[4,64]{1,0:T(4,128)S(1)} %get-tuple-element.77, f32[4,64]{1,0:T(4,128)S(1)} %get-tuple-element.78), channel_id=1, replica_groups=mesh['rows_0'=2,'rows_1'=4,'cols_0'=8,'cols_1'=2,'cols_2'=2] {'cols_0'}, use_global_device_ids=true, to_apply=%region_9.0 | all-reduce | flops 512 | bytes 4096 | tf_op jit(solution)/shard_map/psum | solution.py:15
  45.5 10.9 %all-reduce.11 = (f32[4,64]{1,0:T(4,128)S(1)}, f32[4,64]{1,0:T(4,128)S(1)}) all-reduce(f32[4,64]{1,0:T(4,128)S(1)} %get-tuple-element.93, f32[4,64]{1,0:T(4,128)S(1)} %get-tuple-element.94), channel_id=1, replica_groups=mesh['rows_0'=2,'rows_1'=4,'cols_0'=8,'cols_1'=2,'cols_2'=2] {'cols_2'}, use_global_device_ids=true, to_apply=%region_11.0 | all-reduce | flops 512 | bytes 4096 | tf_op jit(solution)/shard_map/psum | solution.py:15
  66.7 4.5 reshape.237
  87.8 5.0 pad_maximum_fusion
  92.9 4.2 fusion.42
  120.8 10.8 %all-reduce.18 = (f32[4,64]{1,0:T(4,128)S(1)}, f32[4,64]{1,0:T(4,128)S(1)}) all-reduce(f32[4,64]{1,0:T(4,128)S(1)} %get-tuple-element.55, f32[4,64]{1,0:T(4,128)S(1)} %get-tuple-element.54), channel_id=1, replica_groups=mesh['rows_0'=2,'rows_1'=4,'cols_0'=8,'cols_1'=2,'cols_2'=2] {'rows_0'}, use_global_device_ids=true, to_apply=%region_19.0 | all-reduce | flops 512 | bytes 4096 | tf_op jit(solution)/shard_map/psum | solution.py:15
  131.7 7.4 %all-reduce.6 = (f32[4,64]{1,0:T(4,128)S(1)}, f32[4,64]{1,0:T(4,128)S(1)}) all-reduce(f32[4,64]{1,0:T(4,128)S(1)} %get-tuple-element.99, f32[4,64]{1,0:T(4,128)S(1)} %get-tuple-element.100), channel_id=1, replica_groups=mesh['rows_0'=2,'rows_1'=4,'cols_0'=8,'cols_1'=2,'cols_2'=2] {'rows_1'}, use_global_device_ids=true, to_apply=%region_20.0 | all-reduce | flops 512 | bytes 4096 | tf_op jit(solution)/shard_map/psum | solution.py:15
  139.1 10.7 %all-reduce.2 = (f32[4,64]{1,0:T(4,128)S(1)}, f32[4,64]{1,0:T(4,128)S(1)}) all-reduce(f32[4,64]{1,0:T(4,128)S(1)} %get-tuple-element.75, f32[4,64]{1,0:T(4,128)S(1)} %get-tuple-element.76), channel_id=1, replica_groups=mesh['rows_0'=2,'rows_1'=4,'cols_0'=8,'cols_1'=2,'cols_2'=2] {'cols_0'}, use_global_device_ids=true, to_apply=%region_21.0 | all-reduce | flops 512 | bytes 4096 | tf_op jit(solution)/shard_map/psum | solution.py:15
  153.5 12.3 %all-reduce.10 = (f32[4,64]{1,0:T(4,128)S(1)}, f32[4,64]{1,0:T(4,128)S(1)}) all-reduce(f32[4,64]{1,0:T(4,128)S(1)} %get-tuple-element.91, f32[4,64]{1,0:T(4,128)S(1)} %get-tuple-element.92), channel_id=1, replica_groups=mesh['rows_0'=2,'rows_1'=4,'cols_0'=8,'cols_1'=2,'cols_2'=2] {'cols_2'}, use_global_device_ids=true, to_apply=%region_23.0 | all-reduce | flops 512 | bytes 4096 | tf_op jit(solution)/shard_map/psum | solution.py:15
  165.9 4.7 multiply_multiply_fusion
  174.6 5.8 %all-reduce.17 = (f32[4,64]{1,0:T(4,128)S(1)}, f32[4,64]{1,0:T(4,128)}) all-reduce(f32[4,64]{1,0:T(4,128)S(1)} %get-tuple-element.53, f32[4,64]{1,0:T(4,128)S(1)} %get-tuple-element.52), channel_id=1, replica_groups=mesh['rows_0'=2,'rows_1'=4,'cols_0'=8,'cols_1'=2,'cols_2'=2] {'rows_0'}, use_global_device_ids=true, to_apply=%region_31.0 | all-reduce | flops 512 | bytes 4096 | tf_op jit(solution)/shard_map/psum | solution.py:15
  180.4 6.1 %all-reduce.5 = (f32[4,64]{1,0:T(4,128)S(1)}, f32[4,64]{1,0:T(4,128)S(1)}) all-reduce(f32[4,64]{1,0:T(4,128)S(1)} %get-tuple-element.97, f32[4,64]{1,0:T(4,128)} %get-tuple-element.98), channel_id=1, replica_groups=mesh['rows_0'=2,'rows_1'=4,'cols_0'=8,'cols_1'=2,'cols_2'=2] {'rows_1'}, use_global_device_ids=true, to_apply=%region_32.0 | all-reduce | flops 512 | bytes 4096 | tf_op jit(solution)/shard_map/psum | solution.py:15
  186.5 13.4 %all-reduce.1 = (f32[4,64]{1,0:T(4,128)S(1)}, f32[4,64]{1,0:T(4,128)}) all-reduce(f32[4,64]{1,0:T(4,128)S(1)} %get-tuple-element.73, f32[4,64]{1,0:T(4,128)S(1)} %get-tuple-element.74), channel_id=1, replica_groups=mesh['rows_0'=2,'rows_1'=4,'cols_0'=8,'cols_1'=2,'cols_2'=2] {'cols_0'}, use_global_device_ids=true, to_apply=%region_33.0 | all-reduce | flops 512 | bytes 4096 | tf_op jit(solution)/shard_map/psum | solution.py:15
  203.8 10.6 %all-reduce.9 = (f32[4,64]{1,0:T(4,128)S(1)}, f32[4,64]{1,0:T(4,128)}) all-reduce(f32[4,64]{1,0:T(4,128)S(1)} %get-tuple-element.89, f32[4,64]{1,0:T(4,128)S(1)} %get-tuple-element.90), channel_id=1, replica_groups=mesh['rows_0'=2,'rows_1'=4,'cols_0'=8,'cols_1'=2,'cols_2'=2] {'cols_2'}, use_global_device_ids=true, to_apply=%region_35.0 | all-reduce | flops 512 | bytes 4096 | tf_op jit(solution)/shard_map/psum | solution.py:15
  226.9 4.3 collective-permute-start.4
  253.6 5.2 maximum_maximum_fusion.1
  268.8 7.9 %all-reduce.16 = (f32[4,64]{1,0:T(4,128)S(1)}, f32[4,64]{1,0:T(4,128)S(1)}) all-reduce(f32[4,64]{1,0:T(4,128)S(1)} %get-tuple-element.51, f32[4,64]{1,0:T(4,128)S(1)} %get-tuple-element.50), channel_id=1, replica_groups=mesh['rows_0'=2,'rows_1'=4,'cols_0'=8,'cols_1'=2,'cols_2'=2] {'rows_0'}, use_global_device_ids=true, to_apply=%region_43.0 | all-reduce | flops 512 | bytes 4096 | tf_op jit(solution)/shard_map/psum | solution.py:15
  276.7 9.6 %all-reduce.4 = (f32[4,64]{1,0:T(4,128)S(1)}, f32[4,64]{1,0:T(4,128)S(1)}) all-reduce(f32[4,64]{1,0:T(4,128)S(1)} %get-tuple-element.95, f32[4,64]{1,0:T(4,128)S(1)} %get-tuple-element.96), channel_id=1, replica_groups=mesh['rows_0'=2,'rows_1'=4,'cols_0'=8,'cols_1'=2,'cols_2'=2] {'rows_1'}, use_global_device_ids=true, to_apply=%region_44.0 | all-reduce | flops 512 | bytes 4096 | tf_op jit(solution)/shard_map/psum | solution.py:15
  286.2 10.8 %all-reduce = (f32[4,64]{1,0:T(4,128)S(1)}, f32[4,64]{1,0:T(4,128)S(1)}) all-reduce(f32[4,64]{1,0:T(4,128)S(1)} %get-tuple-element.71, f32[4,64]{1,0:T(4,128)S(1)} %get-tuple-element.72), channel_id=1, replica_groups=mesh['rows_0'=2,'rows_1'=4,'cols_0'=8,'cols_1'=2,'cols_2'=2] {'cols_0'}, use_global_device_ids=true, to_apply=%region_45.0 | all-reduce | flops 512 | bytes 4096 | tf_op jit(solution)/shard_map/psum | solution.py:15
  297.0 5.1 all-reduce.12
  302.1 8.7 %all-reduce.8 = (f32[4,64]{1,0:T(4,128)S(1)}, f32[4,64]{1,0:T(4,128)S(1)}) all-reduce(f32[4,64]{1,0:T(4,128)S(1)} %get-tuple-element.87, f32[4,64]{1,0:T(4,128)S(1)} %get-tuple-element.88), channel_id=1, replica_groups=mesh['rows_0'=2,'rows_1'=4,'cols_0'=8,'cols_1'=2,'cols_2'=2] {'cols_2'}, use_global_device_ids=true, to_apply=%region_47.0 | all-reduce | flops 512 | bytes 4096 | tf_op jit(solution)/shard_map/psum | solution.py:15
  320.3 236.9 %all-reduce.22.cloned.1.call-done = f32[72192]{0:T(1024)} async-done(((f32[72192]{0:T(1024)}), f32[72192]{0:T(1024)}) %all-reduce.22.cloned.1.call-update) | async-done | bytes 288784 | tf_op jit(solution)/shard_map/psum | solution.py:37
  (220 shorter events, 131.3 us)
Async XLA Ops:
  7.2 550.0 %all-reduce.22.cloned.1.call-start = ((), (), s32[]{:S(2)}) async-start(), calls=%async_computation | async-start | bytes 581632 | tf_op jit(solution)/shard_map/psum | solution.py:37
  10.1 46.3 %copy-start.39 = (f32[64]{0:T(128)S(1)}, f32[64]{0:T(128)}, u32[]{:S(2)}) copy-start(f32[64]{0:T(128)} %param.22) | copy-start | bytes 772
  10.1 46.3 %copy-start.42 = (f32[64]{0:T(128)S(1)}, f32[64]{0:T(128)}, u32[]{:S(2)}) copy-start(f32[64]{0:T(128)} %param.23) | copy-start | bytes 772
  10.7 47.4 %copy-start = (f32[4,64,1024]{2,1,0:T(8,128)}, f32[4,64,1024]{2,1,0:T(8,128)S(1)}, u32[]{:S(2)}) copy-start(f32[4,64,1024]{2,1,0:T(8,128)S(1)} %get-tuple-element.147) | copy-start | bytes 3145732
  58.2 6.9 %copy-start.38 = (f32[4,64]{1,0:T(4,128)S(1)}, f32[4,64]{1,0:T(4,128)}, u32[]{:S(2)}) copy-start(f32[4,64]{1,0:T(4,128)} %param.19) | copy-start | bytes 3076
  60.0 6.0 %copy-start.37 = (bf16[64,256]{1,0:T(8,128)(2,1)S(1)}, bf16[64,256]{1,0:T(8,128)(2,1)}, u32[]{:S(2)}) copy-start(bf16[64,256]{1,0:T(8,128)(2,1)} %param.17) | copy-start | bytes 98308
  60.8 10.4 %collective-permute-start = (bf16[4,64,1,128]{1,0,3,2:T(4,128)(2,1)}, bf16[4,64,1,128]{1,0,3,2:T(4,128)(2,1)}, u32[]{:S(2)}, u32[]{:S(2)}) collective-permute-start(bf16[4,64,1,128]{1,0,3,2:T(4,128)(2,1)} %get-tuple-element.125), channel_id=1, source_target_pairs={{0,32},{32,64},{64,96},{96,128},{128,160},{160,192},{192,224},{1,3... | collective-permute-start | bytes 196616 | tf_op jit(solution)/shard_map/ppermute | solution.py:26
  62.8 8.5 %collective-permute-start.1 = (bf16[4,64,1,128]{1,0,3,2:T(4,128)(2,1)}, bf16[4,64,1,128]{1,0,3,2:T(4,128)(2,1)}, u32[]{:S(2)}, u32[]{:S(2)}) collective-permute-start(bf16[4,64,1,128]{1,0,3,2:T(4,128)(2,1)} %get-tuple-element.126), channel_id=1, source_target_pairs={{32,0},{64,32},{96,64},{128,96},{160,128},{192,160},{224,192},{33,... | collective-permute-start | bytes 196616 | tf_op jit(solution)/shard_map/ppermute | solution.py:28
  71.9 15.9 %collective-permute-start.2 = (bf16[4,64,10,1]{1,0,3,2:T(4,128)(2,1)S(1)}, bf16[4,64,10,1]{1,0,3,2:T(4,128)(2,1)S(1)}, u32[]{:S(2)}, u32[]{:S(2)}) collective-permute-start(bf16[4,64,10,1]{1,0,3,2:T(4,128)(2,1)S(1)} %get-tuple-element.122), channel_id=1, source_target_pairs={{0,1},{1,2},{2,3},{3,4},{4,5},{5,6},{6,7},{7,8},{8,9},{9,10},{10,1... | collective-permute-start | bytes 15368 | tf_op jit(solution)/shard_map/ppermute | solution.py:26
  75.5 12.4 %collective-permute-start.3 = (bf16[4,64,10,1]{1,0,3,2:T(4,128)(2,1)S(1)}, bf16[4,64,10,1]{1,0,3,2:T(4,128)(2,1)S(1)}, u32[]{:S(2)}, u32[]{:S(2)}) collective-permute-start(bf16[4,64,10,1]{1,0,3,2:T(4,128)(2,1)S(1)} %get-tuple-element.121), channel_id=1, source_target_pairs={{1,0},{2,1},{3,2},{4,3},{5,4},{6,5},{7,6},{8,7},{9,8},{10,9},{11,1... | collective-permute-start | bytes 15368 | tf_op jit(solution)/shard_map/ppermute | solution.py:28
  98.7 4.8 copy-start.6
  98.7 4.8 copy-start.4
  119.6 46.2 %copy-start.44 = (f32[64]{0:T(128)S(1)}, f32[64]{0:T(128)}, u32[]{:S(2)}) copy-start(f32[64]{0:T(128)} %param.24) | copy-start | bytes 772
  165.8 4.7 copy-start.24
  165.8 4.7 copy-start.33
  165.8 4.7 copy-start.45
  165.8 4.7 copy-start.46
  165.8 4.7 copy-start.47
  226.1 8.8 %copy-start.34 = (f32[64,256]{1,0:T(8,128)S(1)}, f32[64,256]{1,0:T(8,128)}, u32[]{:S(2)}) copy-start(f32[64,256]{1,0:T(8,128)} %get-tuple-element.60) | copy-start | bytes 196612
  226.9 10.6 %collective-permute-start.4 = (bf16[4,64,1,128]{1,0,3,2:T(4,128)(2,1)}, bf16[4,64,1,128]{1,0,3,2:T(4,128)(2,1)}, u32[]{:S(2)}, u32[]{:S(2)}) collective-permute-start(bf16[4,64,1,128]{1,0,3,2:T(4,128)(2,1)} %get-tuple-element.123), channel_id=1, source_target_pairs={{0,32},{32,64},{64,96},{96,128},{128,160},{160,192},{192,224},{1,3... | collective-permute-start | bytes 196616 | tf_op jit(solution)/shard_map/ppermute | solution.py:26
  231.2 5.7 copy-start.41
  231.2 6.8 %collective-permute-start.5 = (bf16[4,64,1,128]{1,0,3,2:T(4,128)(2,1)}, bf16[4,64,1,128]{1,0,3,2:T(4,128)(2,1)}, u32[]{:S(2)}, u32[]{:S(2)}) collective-permute-start(bf16[4,64,1,128]{1,0,3,2:T(4,128)(2,1)} %get-tuple-element.124), channel_id=1, source_target_pairs={{32,0},{64,32},{96,64},{128,96},{160,128},{192,160},{224,192},{33,... | collective-permute-start | bytes 196616 | tf_op jit(solution)/shard_map/ppermute | solution.py:28
  238.7 15.0 %collective-permute-start.6 = (bf16[4,64,10,1]{1,0,3,2:T(4,128)(2,1)S(1)}, bf16[4,64,10,1]{1,0,3,2:T(4,128)(2,1)S(1)}, u32[]{:S(2)}, u32[]{:S(2)}) collective-permute-start(bf16[4,64,10,1]{1,0,3,2:T(4,128)(2,1)S(1)} %get-tuple-element.118), channel_id=1, source_target_pairs={{1,0},{2,1},{3,2},{4,3},{5,4},{6,5},{7,6},{8,7},{9,8},{10,9},{11,1... | collective-permute-start | bytes 15368 | tf_op jit(solution)/shard_map/ppermute | solution.py:28
  242.1 11.6 %collective-permute-start.7 = (bf16[4,64,10,1]{1,0,3,2:T(4,128)(2,1)S(1)}, bf16[4,64,10,1]{1,0,3,2:T(4,128)(2,1)S(1)}, u32[]{:S(2)}, u32[]{:S(2)}) collective-permute-start(bf16[4,64,10,1]{1,0,3,2:T(4,128)(2,1)S(1)} %get-tuple-element.117), channel_id=1, source_target_pairs={{0,1},{1,2},{2,3},{3,4},{4,5},{5,6},{6,7},{7,8},{8,9},{9,10},{10,1... | collective-permute-start | bytes 15368 | tf_op jit(solution)/shard_map/ppermute | solution.py:26
  (34 other events, 49.5 us)
Sparse Core Ops, SparseCore 0:
  315.0 242.1 all-reduce.21
where the time goes:
time: 575 us; the launch traced here: 572 us
  waiting for transfers between devices  237 us (41%)
  blocking collectives  172 us (30%)
  local copies, waits for them, and re-layouts  71 us (12%)
  other arithmetic  28.2 us (5%)
  matrix products  28 us (5%)
  starting transfers between devices  20.1 us (3%)
  between operations  14.9 us (3%)
    psum x1, waiting for transfers between devices, packed_total(): so_far = lax.psum(flat, axis)  237 us
    psum x20, blocking collectives, by_axis(): return functools.reduce(lax.psum, axes, array)  172 us
    reshape x8, local copies, waits for them, and re-layouts, conv_forward(): padded[:, :, row_off:row_off + tall, col_off:col_off + broad]  17.3 us
    concatenate x6, other arithmetic, with_halo(): jnp.concatenate([lax.ppermute(tail, axis, [(i, (i + 1) % count) for i in...  17.3 us
    unnamed x111, local copies, waits for them, and re-layouts  13.8 us
    ppermute x4, starting transfers between devices, with_halo(): lax.ppermute(tail, axis, [(i, (i + 1) % count) for i in range(ends)])  12.1 us
  transfers between devices with their start and end apart: 9, of which 2 were waited for; matrix products, arithmetic and copies ran while one was open for 6% of the time, Pallas kernels for 0%

commit v1 on v0

--- a/solution.py
+++ b/solution.py
@@ -34,7 +34,8 @@
 
 def packed_total(arrays, axis):
     flat, at, finished = (jnp.concatenate([a.reshape(-1) for a in arrays]), 0, [])
-    so_far = lax.psum(flat, axis)
+    blocks = lax.all_gather(flat, axis, axis=0, tiled=False)
+    so_far = blocks.sum(axis=0)
     for a in arrays:
         finished.append(so_far[at : at + a.size].reshape(a.shape))
         at += a.size

time: 575 us -> 860 us (1.50)
  waiting for transfers between devices: 237 us -> 472 us
  other arithmetic: 28.2 us -> 78.8 us
    all_gather x0 -> x1, waiting for transfers between devices: none -> 472 us  [packed_total(): blocks = lax.all_gather(flat, axis, axis=0, tiled=False)]
    psum x1 -> x0, waiting for transfers between devices: 237 us -> none  [packed_total(): so_far = lax.psum(flat, axis)]
    reduce_sum x0 -> x1, other arithmetic: none -> 49.7 us  [packed_total(): so_far = blocks.sum(axis=0)]
  transfers between devices with their start and end apart: 9 -> 9, of which waited for: 2 -> 1; matrix products, arithmetic and copies ran while one was open for 6% -> 4% of each run, Pallas kernels for 0% -> 0%
where the time goes in v1:
time: 860 us; the launch traced here: 857 us
  waiting for transfers between devices  472 us (55%)
  blocking collectives  175 us (20%)
  other arithmetic  78.8 us (9%)
  local copies, waits for them, and re-layouts  70.8 us (8%)
  matrix products  25.5 us (3%)
  starting transfers between devices  20 us (2%)
  between operations  14.9 us (2%)
    all_gather x1, waiting for transfers between devices, packed_total(): blocks = lax.all_gather(flat, axis, axis=0, tiled=False)  472 us
    psum x20, blocking collectives, by_axis(): return functools.reduce(lax.psum, axes, array)  175 us
    reduce_sum x1, other arithmetic, packed_total(): so_far = blocks.sum(axis=0)  49.7 us
    concatenate x6, other arithmetic, with_halo(): jnp.concatenate([lax.ppermute(tail, axis, [(i, (i + 1) % count) for i in...  17.4 us
  transfers between devices with their start and end apart: 9, of which 1 were waited for; matrix products, arithmetic and copies ran while one was open for 4% of the time, Pallas kernels for 0%

profile of v1, /device:TPU:1, one launch (start us, length us, event | category | flops | bytes accessed | tf_op | source)
XLA Modules:
  0.0 856.6 jit_solution(6580595784243290432)
XLA Ops:
  11.5 5.9 all-reduce.19
  17.4 8.9 %all-reduce.7 = (f32[4,64]{1,0:T(4,128)S(1)}, f32[4,64]{1,0:T(4,128)S(1)}) all-reduce(f32[4,64]{1,0:T(4,128)S(1)} %get-tuple-element.101, f32[4,64]{1,0:T(4,128)S(1)} %get-tuple-element.102), channel_id=1, replica_groups=mesh['rows_0'=2,'rows_1'=4,'cols_0'=8,'cols_1'=2,'cols_2'=2] {'rows_1'}, use_global_device_ids=true, to_apply=%region_8.0 | all-reduce | flops 512 | bytes 4096 | tf_op jit(solution)/shard_map/psum | solution.py:15
  26.3 16.2 %all-reduce.3 = (f32[4,64]{1,0:T(4,128)S(1)}, f32[4,64]{1,0:T(4,128)S(1)}) all-reduce(f32[4,64]{1,0:T(4,128)S(1)} %get-tuple-element.77, f32[4,64]{1,0:T(4,128)S(1)} %get-tuple-element.78), channel_id=1, replica_groups=mesh['rows_0'=2,'rows_1'=4,'cols_0'=8,'cols_1'=2,'cols_2'=2] {'cols_0'}, use_global_device_ids=true, to_apply=%region_9.0 | all-reduce | flops 512 | bytes 4096 | tf_op jit(solution)/shard_map/psum | solution.py:15
  46.3 10.9 %all-reduce.11 = (f32[4,64]{1,0:T(4,128)S(1)}, f32[4,64]{1,0:T(4,128)S(1)}) all-reduce(f32[4,64]{1,0:T(4,128)S(1)} %get-tuple-element.93, f32[4,64]{1,0:T(4,128)S(1)} %get-tuple-element.94), channel_id=1, replica_groups=mesh['rows_0'=2,'rows_1'=4,'cols_0'=8,'cols_1'=2,'cols_2'=2] {'cols_2'}, use_global_device_ids=true, to_apply=%region_11.0 | all-reduce | flops 512 | bytes 4096 | tf_op jit(solution)/shard_map/psum | solution.py:15
  67.5 4.5 reshape.237
  88.8 5.0 pad_maximum_fusion
  119.7 10.9 %all-reduce.18 = (f32[4,64]{1,0:T(4,128)S(1)}, f32[4,64]{1,0:T(4,128)S(1)}) all-reduce(f32[4,64]{1,0:T(4,128)S(1)} %get-tuple-element.55, f32[4,64]{1,0:T(4,128)S(1)} %get-tuple-element.54), channel_id=1, replica_groups=mesh['rows_0'=2,'rows_1'=4,'cols_0'=8,'cols_1'=2,'cols_2'=2] {'rows_0'}, use_global_device_ids=true, to_apply=%region_19.0 | all-reduce | flops 512 | bytes 4096 | tf_op jit(solution)/shard_map/psum | solution.py:15
  130.6 7.3 all-reduce.6
  137.9 11.0 %all-reduce.2 = (f32[4,64]{1,0:T(4,128)S(1)}, f32[4,64]{1,0:T(4,128)S(1)}) all-reduce(f32[4,64]{1,0:T(4,128)S(1)} %get-tuple-element.75, f32[4,64]{1,0:T(4,128)S(1)} %get-tuple-element.76), channel_id=1, replica_groups=mesh['rows_0'=2,'rows_1'=4,'cols_0'=8,'cols_1'=2,'cols_2'=2] {'cols_0'}, use_global_device_ids=true, to_apply=%region_21.0 | all-reduce | flops 512 | bytes 4096 | tf_op jit(solution)/shard_map/psum | solution.py:15
  152.9 9.9 %all-reduce.10 = (f32[4,64]{1,0:T(4,128)S(1)}, f32[4,64]{1,0:T(4,128)S(1)}) all-reduce(f32[4,64]{1,0:T(4,128)S(1)} %get-tuple-element.91, f32[4,64]{1,0:T(4,128)S(1)} %get-tuple-element.92), channel_id=1, replica_groups=mesh['rows_0'=2,'rows_1'=4,'cols_0'=8,'cols_1'=2,'cols_2'=2] {'cols_2'}, use_global_device_ids=true, to_apply=%region_23.0 | all-reduce | flops 512 | bytes 4096 | tf_op jit(solution)/shard_map/psum | solution.py:15
  162.9 4.7 multiply_multiply_fusion
  171.6 5.8 all-reduce.17
  177.5 6.7 all-reduce.5
  184.1 12.4 %all-reduce.1 = (f32[4,64]{1,0:T(4,128)}, f32[4,64]{1,0:T(4,128)}) all-reduce(f32[4,64]{1,0:T(4,128)S(1)} %get-tuple-element.73, f32[4,64]{1,0:T(4,128)S(1)} %get-tuple-element.74), channel_id=1, replica_groups=mesh['rows_0'=2,'rows_1'=4,'cols_0'=8,'cols_1'=2,'cols_2'=2] {'cols_0'}, use_global_device_ids=true, to_apply=%region_33.0 | all-reduce | flops 512 | bytes 4096 | tf_op jit(solution)/shard_map/psum | solution.py:15
  196.5 4.5 all-reduce.13
  201.0 10.8 %all-reduce.9 = (f32[4,64]{1,0:T(4,128)S(1)}, f32[4,64]{1,0:T(4,128)}) all-reduce(f32[4,64]{1,0:T(4,128)S(1)} %get-tuple-element.89, f32[4,64]{1,0:T(4,128)} %get-tuple-element.90), channel_id=1, replica_groups=mesh['rows_0'=2,'rows_1'=4,'cols_0'=8,'cols_1'=2,'cols_2'=2] {'cols_2'}, use_global_device_ids=true, to_apply=%region_35.0 | all-reduce | flops 512 | bytes 4096 | tf_op jit(solution)/shard_map/psum | solution.py:15
  225.0 4.3 collective-permute-start.4
  251.6 5.3 maximum_maximum_fusion.1
  267.2 8.4 all-reduce.16
  275.7 9.1 %all-reduce.4 = (f32[4,64]{1,0:T(4,128)S(1)}, f32[4,64]{1,0:T(4,128)S(1)}) all-reduce(f32[4,64]{1,0:T(4,128)S(1)} %get-tuple-element.95, f32[4,64]{1,0:T(4,128)S(1)} %get-tuple-element.96), channel_id=1, replica_groups=mesh['rows_0'=2,'rows_1'=4,'cols_0'=8,'cols_1'=2,'cols_2'=2] {'rows_1'}, use_global_device_ids=true, to_apply=%region_44.0 | all-reduce | flops 512 | bytes 4096 | tf_op jit(solution)/shard_map/psum | solution.py:15
  284.8 11.5 %all-reduce = (f32[4,64]{1,0:T(4,128)S(1)}, f32[4,64]{1,0:T(4,128)S(1)}) all-reduce(f32[4,64]{1,0:T(4,128)S(1)} %get-tuple-element.71, f32[4,64]{1,0:T(4,128)S(1)} %get-tuple-element.72), channel_id=1, replica_groups=mesh['rows_0'=2,'rows_1'=4,'cols_0'=8,'cols_1'=2,'cols_2'=2] {'cols_0'}, use_global_device_ids=true, to_apply=%region_45.0 | all-reduce | flops 512 | bytes 4096 | tf_op jit(solution)/shard_map/psum | solution.py:15
  300.1 12.8 %all-reduce.8 = (f32[4,64]{1,0:T(4,128)S(1)}, f32[4,64]{1,0:T(4,128)S(1)}) all-reduce(f32[4,64]{1,0:T(4,128)S(1)} %get-tuple-element.87, f32[4,64]{1,0:T(4,128)S(1)} %get-tuple-element.88), channel_id=1, replica_groups=mesh['rows_0'=2,'rows_1'=4,'cols_0'=8,'cols_1'=2,'cols_2'=2] {'cols_2'}, use_global_device_ids=true, to_apply=%region_47.0 | all-reduce | flops 512 | bytes 4096 | tf_op jit(solution)/shard_map/psum | solution.py:15
  323.1 472.0 %all-gather.4.cloned.1.call-done = f32[256,1,72192]{2,1,0:T(1,128)} async-done(((f32[1,1,72192]{2,1,0:T(1,128)}), f32[256,1,72192]{2,1,0:T(1,128)}) %all-gather.4.cloned.1.call-update) | async-done | bytes 73924624 | tf_op jit(solution)/shard_map/all_gather | solution.py:37
  795.1 49.7 %reduce_sum.195 = f32[72192]{0:T(1024)S(1)} reduce(f32[256,1,72192]{2,1,0:T(1,128)} %all-gather.4.cloned.1.call-done, f32[]{:T(128)} %constant.16.clone.1), dimensions={0,1}, to_apply=%region_55.0 | reduce | flops 18408960 | bytes 74213376 | tf_op jit(solution)/shard_map/reduce_sum | solution.py:38
  (222 shorter events, 133.2 us)
Async XLA Ops:
  7.2 787.9 %all-gather.4.cloned.1.call-start = ((), (), s32[]{:S(2)}) async-start(), calls=%async_computation | async-start | bytes 74213376 | tf_op jit(solution)/shard_map/all_gather | solution.py:37
  10.9 46.3 %copy-start.40 = (f32[64]{0:T(128)S(1)}, f32[64]{0:T(128)}, u32[]{:S(2)}) copy-start(f32[64]{0:T(128)} %param.22) | copy-start | bytes 772
  10.9 46.3 %copy-start.42 = (f32[64]{0:T(128)S(1)}, f32[64]{0:T(128)}, u32[]{:S(2)}) copy-start(f32[64]{0:T(128)} %param.23) | copy-start | bytes 772
  11.5 47.4 %copy-start = (f32[4,64,1024]{2,1,0:T(8,128)}, f32[4,64,1024]{2,1,0:T(8,128)S(1)}, u32[]{:S(2)}) copy-start(f32[4,64,1024]{2,1,0:T(8,128)S(1)} %get-tuple-element.147) | copy-start | bytes 3145732
  58.9 6.9 copy-start.37
  60.8 6.0 copy-start.36
  61.6 10.4 %collective-permute-start = (bf16[4,64,1,128]{1,0,3,2:T(4,128)(2,1)}, bf16[4,64,1,128]{1,0,3,2:T(4,128)(2,1)}, u32[]{:S(2)}, u32[]{:S(2)}) collective-permute-start(bf16[4,64,1,128]{1,0,3,2:T(4,128)(2,1)} %get-tuple-element.125), channel_id=1, source_target_pairs={{0,32},{32,64},{64,96},{96,128},{128,160},{160,192},{192,224},{1,3... | collective-permute-start | bytes 196616 | tf_op jit(solution)/shard_map/ppermute | solution.py:26
  63.5 8.4 collective-permute-start.1
  72.7 16.1 %collective-permute-start.3 = (bf16[4,64,10,1]{1,0,3,2:T(4,128)(2,1)S(1)}, bf16[4,64,10,1]{1,0,3,2:T(4,128)(2,1)S(1)}, u32[]{:S(2)}, u32[]{:S(2)}) collective-permute-start(bf16[4,64,10,1]{1,0,3,2:T(4,128)(2,1)S(1)} %get-tuple-element.121), channel_id=1, source_target_pairs={{1,0},{2,1},{3,2},{4,3},{5,4},{6,5},{7,6},{8,7},{9,8},{10,9},{11,1... | collective-permute-start | bytes 15368 | tf_op jit(solution)/shard_map/ppermute | solution.py:28
  75.1 13.7 %collective-permute-start.2 = (bf16[4,64,10,1]{1,0,3,2:T(4,128)(2,1)S(1)}, bf16[4,64,10,1]{1,0,3,2:T(4,128)(2,1)S(1)}, u32[]{:S(2)}, u32[]{:S(2)}) collective-permute-start(bf16[4,64,10,1]{1,0,3,2:T(4,128)(2,1)S(1)} %get-tuple-element.122), channel_id=1, source_target_pairs={{0,1},{1,2},{2,3},{3,4},{4,5},{5,6},{6,7},{7,8},{8,9},{9,10},{10,1... | collective-permute-start | bytes 15368 | tf_op jit(solution)/shard_map/ppermute | solution.py:26
  105.3 4.8 copy-start.6
  105.3 4.8 copy-start.4
  118.5 44.4 %copy-start.44 = (f32[64]{0:T(128)S(1)}, f32[64]{0:T(128)}, u32[]{:S(2)}) copy-start(f32[64]{0:T(128)} %param.24) | copy-start | bytes 772
  162.9 4.7 copy-start.25
  162.9 4.7 copy-start.33
  162.9 4.7 copy-start.46
  162.9 4.7 copy-start.47
  162.9 4.7 copy-start.48
  211.7 3.2 copy-start.7
  224.2 9.3 %copy-start.34 = (f32[64,256]{1,0:T(8,128)S(1)}, f32[64,256]{1,0:T(8,128)}, u32[]{:S(2)}) copy-start(f32[64,256]{1,0:T(8,128)} %get-tuple-element.60) | copy-start | bytes 196612
  225.0 11.0 %collective-permute-start.4 = (bf16[4,64,1,128]{1,0,3,2:T(4,128)(2,1)}, bf16[4,64,1,128]{1,0,3,2:T(4,128)(2,1)}, u32[]{:S(2)}, u32[]{:S(2)}) collective-permute-start(bf16[4,64,1,128]{1,0,3,2:T(4,128)(2,1)} %get-tuple-element.123), channel_id=1, source_target_pairs={{0,32},{32,64},{64,96},{96,128},{128,160},{160,192},{192,224},{1,3... | collective-permute-start | bytes 196616 | tf_op jit(solution)/shard_map/ppermute | solution.py:26
  229.3 6.8 collective-permute-start.5
  236.8 14.8 %collective-permute-start.7 = (bf16[4,64,10,1]{1,0,3,2:T(4,128)(2,1)S(1)}, bf16[4,64,10,1]{1,0,3,2:T(4,128)(2,1)S(1)}, u32[]{:S(2)}, u32[]{:S(2)}) collective-permute-start(bf16[4,64,10,1]{1,0,3,2:T(4,128)(2,1)S(1)} %get-tuple-element.117), channel_id=1, source_target_pairs={{0,1},{1,2},{2,3},{3,4},{4,5},{5,6},{6,7},{7,8},{8,9},{9,10},{10,1... | collective-permute-start | bytes 15368 | tf_op jit(solution)/shard_map/ppermute | solution.py:26
  240.3 11.3 %collective-permute-start.6 = (bf16[4,64,10,1]{1,0,3,2:T(4,128)(2,1)S(1)}, bf16[4,64,10,1]{1,0,3,2:T(4,128)(2,1)S(1)}, u32[]{:S(2)}, u32[]{:S(2)}) collective-permute-start(bf16[4,64,10,1]{1,0,3,2:T(4,128)(2,1)S(1)} %get-tuple-element.118), channel_id=1, source_target_pairs={{1,0},{2,1},{3,2},{4,3},{5,4},{6,5},{7,6},{8,7},{9,8},{10,9},{11,1... | collective-permute-start | bytes 15368 | tf_op jit(solution)/shard_map/ppermute | solution.py:28
  (34 other events, 45.7 us)
Sparse Core Ops, SparseCore 0:
  317.3 477.8 all-gather.3
